TPU v7x, 32 devices: a whole 2x2x4 slice. The times are simulated.
32 devices in a mesh: lat: 8 (over y, x, core), lon: 4 (over z).
Axes of the slice: x: 2, y: 2, z: 4, core: 2. Of those that a mesh axis runs over, the one named last changes fastest.
Arguments:
- right_side: float32 [256, 4096], P('lat', 'lon'), may hold values from -6 to 6
- coefficients: float32 [4, 256, 4096], P(None, 'lat', 'lon'), may hold values from 0.2 to 1.2
- extra: float32 [256, 4096], P('lat', 'lon'), may hold values from 0.05 to 1
- land_mask: int32 [256, 4096], P('lat', 'lon'), may hold values 0 or 1
Outputs:
- solution_field: float32 [256, 4096], P('lat', 'lon')
- residual: float32 [256, 4096], P('lat', 'lon')
- norms: float32 [3], replicated
All inputs are finite; a program needn't handle non-finite values. No bound on the sum of `land_mask` on one device may be relied on, other than what follows from the above.
Results may differ from a plain program's by a relative error of at most 0.00028.
Values sent between devices are 32-bit elements; how exact they have to be, the bound alone decides.
A program may use at most 64 MiB of HBM per device.

v0:
```python
import jax
import jax.numpy as jnp
from jax import lax
from jax.sharding import PartitionSpec as P

DEG = 4
ITERS = 3


LOW_EIG = 0.25
HIGH_EIG = 20.5


def padded_2(block, sides, width):
    for axis, dim in sides:
        count = lax.axis_size(axis)
        forward = [(i, i + 1) for i in range(count - 1)]
        forward.append((count - 1, 0))
        backward = [(target, source) for source, target in forward]
        low = lax.ppermute(
            lax.slice_in_dim(block, block.shape[dim] - width, None, axis=dim), axis, forward
        )
        high = lax.ppermute(lax.slice_in_dim(block, 0, width, axis=dim), axis, backward)
        block = jnp.concatenate([low, block, high], axis=dim)
    return block


def window(a, offset, di, dj, rows_out, cols_out):
    return a[offset + di : offset + di + rows_out, offset + dj : offset + dj + cols_out]


def shrink(a, by):
    return a[by : a.shape[0] - by, by : a.shape[1] - by]


def operate(v, k, depth, diag, links):
    le, ln, lne, lnw = links
    inner = k - 1
    rows_out = v.shape[0] - 2
    cols_out = v.shape[1] - 2
    lo = depth - inner

    def cell(di, dj):
        return window(v, 1, di, dj, rows_out, cols_out)

    def link(a, di, dj):
        return window(a, lo, di, dj, rows_out, cols_out)

    out = window(diag, depth - 1 - inner, 0, 0, rows_out, cols_out) * cell(0, 0)
    out = out - link(le, 0, 0) * cell(0, 1) - link(le, 0, -1) * cell(0, -1)
    out = out - link(ln, 0, 0) * cell(1, 0) - link(ln, -1, 0) * cell(-1, 0)
    out = out - link(lne, 0, 0) * cell(1, 1) - link(lne, -1, -1) * cell(-1, -1)
    out = out - link(lnw, 0, 0) * cell(1, -1) - link(lnw, -1, 1) * cell(-1, 1)
    return out


def chebyshev(r, start, matvec):
    theta = (HIGH_EIG + LOW_EIG) / 2.0
    delta = (HIGH_EIG - LOW_EIG) / 2.0
    sigma = theta / delta
    rho = 1.0 / sigma
    step = r / theta
    z = step
    level_now = start
    for level in range(DEG - 1):
        image, level_new = matvec(z, level_now)
        by = level_now - level_new
        q = shrink(r, by) - image
        rho_new = 1.0 / (2.0 * sigma - rho)
        step = rho_new * rho * shrink(step, by) + 2.0 * rho_new / delta * q
        z = shrink(z, by) + step
        r = shrink(r, by)
        rho = rho_new
        level_now = level_new
    return (z, level_now)


def on_device(right_side, coefficients, extra, land_mask):
    rows_dev, cols_dev = right_side.shape
    depth = DEG
    mask_float = land_mask.astype(jnp.float32)
    fields = jnp.concatenate([coefficients, extra[None], mask_float[None]], 0)
    padded = padded_2(fields, (("lat", 1), ("lon", 2)), depth + 1)
    mp = padded[5]
    mc = mp[1:-1, 1:-1]
    total_rows = rows_dev * lax.axis_size("lat")
    global_rows = (
        lax.axis_index("lat") * rows_dev - depth + jnp.arange(rows_dev + 2 * depth, dtype=jnp.int32)
    )
    keep = (global_rows % total_rows != total_rows - 1).astype(jnp.float32)[:, None]
    le = padded[0][1:-1, 1:-1] * mc * mp[1:-1, 2:]
    ln = padded[1][1:-1, 1:-1] * mc * mp[2:, 1:-1] * keep
    lne = padded[2][1:-1, 1:-1] * mc * mp[2:, 2:] * keep
    lnw = padded[3][1:-1, 1:-1] * mc * mp[2:, :-2] * keep
    diag = padded[4][2:-2, 2:-2] + le[1:-1, 1:-1] + le[1:-1, :-2] + ln[1:-1, 1:-1] + ln[:-2, 1:-1]
    diag = diag + lne[1:-1, 1:-1] + lne[:-2, :-2] + lnw[1:-1, 1:-1] + lnw[:-2, 2:]
    links = (le, ln, lne, lnw)

    def local_matvec(v, k):
        return (operate(v, k, depth, diag, links), k - 1)

    def precondition(r):
        wide = padded_2(r, (("lat", 0), ("lon", 1)), depth)
        z, level_now = chebyshev(wide, depth, local_matvec)
        w = operate(z, level_now, depth, diag, links)
        return (shrink(z, level_now), w)

    def products(r, u, w):
        return lax.psum((jnp.sum(r * u), jnp.sum(w * u), jnp.sum(r * r)), ("lat", "lon"))

    r = mask_float * right_side
    x = jnp.zeros_like(r)
    u, w = precondition(r)
    gamma, dlt, first = products(r, u, w)
    norms = [first]
    alpha = gamma / dlt
    p = u
    s = w
    beta = jnp.float32(0.0)
    for k in range(ITERS):
        if k > 0:
            p = u + beta * p
            s = w + beta * s
        x = x + alpha * p
        r = r - alpha * s
        if k < ITERS - 1:
            u, w = precondition(r)
            gamma_new, dlt, squares = products(r, u, w)
            norms.append(squares)
            beta = gamma_new / gamma
            alpha = gamma_new / (dlt - beta * gamma_new / alpha)
            gamma = gamma_new
    return (x, r, jnp.stack(norms))


def solution(mesh):
    return jax.shard_map(
        on_device,
        mesh=mesh,
        in_specs=(P("lat", "lon"), P(None, "lat", "lon"), P("lat", "lon"), P("lat", "lon")),
        out_specs=(P("lat", "lon"), P("lat", "lon"), P()),
        check_vma=False,
    )
```

profile of v0, /device:TPU:0, one launch (start us, length us, event | category | flops | bytes accessed | tf_op | source)
XLA Modules:
  0.0 193.3 jit_solution(159668076188954365)
XLA Ops:
  0.6 1.0 convert_multiply_fusion
  1.7 0.5 collective-permute-start
  2.2 2.9 %collective-permute-start.1 = (f32[4,1024]{1,0:T(4,128)S(1)}, f32[4,1024]{1,0:T(4,128)S(1)}, u32[]{:S(2)}, u32[]{:S(2)}) collective-permute-start(f32[4,1024]{1,0:T(4,128)S(1)} %get-tuple-element.62), channel_id=1, source_target_pairs={{4,0},{8,4},{12,8},{16,12},{20,16},{24,20},{28,24},{0,28},{5,1},{9... | collective-permute-start | bytes 49160 | tf_op jit(solution)/shard_map/ppermute | solution.py:23
  5.2 0.9 convert_bitcast_fusion
  6.1 1.0 pad_maximum_fusion.3
  7.2 2.6 %collective-permute-start.5 = (f32[6,5,1024]{2,1,0:T(8,128)S(1)}, f32[6,5,1024]{2,1,0:T(8,128)S(1)}, u32[]{:S(2)}, u32[]{:S(2)}) collective-permute-start(f32[6,5,1024]{2,1,0:T(8,128)S(1)} %get-tuple-element.46), channel_id=1, source_target_pairs={{4,0},{8,4},{12,8},{16,12},{20,16},{24,20},{28,24},{0,28},{5,1},{9... | collective-permute-start | bytes 368648 | tf_op jit(solution)/shard_map/ppermute | solution.py:23
  9.9 2.3 %collective-permute-start.2 = (f32[40,4]{1,0:T(8,128)S(1)}, f32[40,4]{1,0:T(8,128)S(1)}, u32[]{:S(2)}, u32[]{:S(2)}) collective-permute-start(f32[40,4]{1,0:T(8,128)S(1)} %get-tuple-element.56), channel_id=1, source_target_pairs={{0,1},{1,2},{2,3},{3,0},{4,5},{5,6},{6,7},{7,4},{8,9},{9,10},{10,1... | collective-permute-start | bytes 1928 | tf_op jit(solution)/shard_map/ppermute | solution.py:20
  12.2 2.1 %collective-permute-start.3 = (f32[40,4]{1,0:T(8,128)S(1)}, f32[40,4]{1,0:T(8,128)S(1)}, u32[]{:S(2)}, u32[]{:S(2)}) collective-permute-start(f32[40,4]{1,0:T(8,128)S(1)} %get-tuple-element.55), channel_id=1, source_target_pairs={{1,0},{2,1},{3,2},{0,3},{5,4},{6,5},{7,6},{4,7},{9,8},{10,9},{11,1... | collective-permute-start | bytes 1928 | tf_op jit(solution)/shard_map/ppermute | solution.py:23
  14.3 1.8 collective-permute-done.2
  16.2 0.1 concatenate.28
  16.4 0.2 pad_maximum_fusion
  16.7 1.4 collective-permute-start.6
  18.1 2.5 %collective-permute-start.7 = (f32[6,42,5]{2,1,0:T(8,128)S(1)}, f32[6,42,5]{2,1,0:T(8,128)S(1)}, u32[]{:S(2)}, u32[]{:S(2)}) collective-permute-start(f32[6,42,5]{2,1,0:T(8,128)S(1)} %get-tuple-element.43), channel_id=1, source_target_pairs={{1,0},{2,1},{3,2},{0,3},{5,4},{6,5},{7,6},{4,7},{9,8},{10,9},{11,1... | collective-permute-start | bytes 15128 | tf_op jit(solution)/shard_map/ppermute | solution.py:23
  20.6 4.7 %collective-permute-done.6 = f32[6,42,5]{2,1,0:T(8,128)S(1)} collective-permute-done((f32[6,42,5]{2,1,0:T(8,128)S(1)}, f32[6,42,5]{2,1,0:T(8,128)S(1)}, u32[]{:S(2)}, u32[]{:S(2)}) %collective-permute-start.6) | collective-permute-done | bytes 5072 | tf_op jit(solution)/shard_map/ppermute | solution.py:20
  25.3 1.3 collective-permute-done.7
  26.6 0.9 concatenate.31
  27.6 0.5 fusion.104
  28.0 0.4 copy-done.1
  28.5 0.8 slice_add_fusion.6
  29.3 0.9 slice_add_fusion.5
  30.2 0.9 fusion.72
  31.1 1.2 multiply_reduce_fusion.7
  32.3 39.0 %all-reduce.2 = (f32[]{:T(128)}, f32[]{:T(128)}) all-reduce(f32[]{:T(128)} %get-tuple-element.8, f32[]{:T(128)} %get-tuple-element.7), channel_id=1, replica_groups=mesh['lat'=8,'lon'=4] {'lat','lon'}, use_global_device_ids=true, to_apply=%region_1.2 | all-reduce | flops 2 | bytes 16 | tf_op jit(solution)/shard_map/psum | solution.py:109
  72.8 2.6 %collective-permute-start.9 = (f32[4,1024]{1,0:T(4,128)S(1)}, f32[4,1024]{1,0:T(4,128)S(1)}, u32[]{:S(2)}, u32[]{:S(2)}) collective-permute-start(f32[4,1024]{1,0:T(4,128)S(1)} %get-tuple-element.60), channel_id=1, source_target_pairs={{4,0},{8,4},{12,8},{16,12},{20,16},{24,20},{28,24},{0,28},{5,1},{9... | collective-permute-start | bytes 49160 | tf_op jit(solution)/shard_map/ppermute | solution.py:23
  75.5 1.4 collective-permute-done.8
  77.0 0.9 collective-permute-start.10
  77.9 2.9 %collective-permute-start.11 = (f32[40,4]{1,0:T(8,128)S(1)}, f32[40,4]{1,0:T(8,128)S(1)}, u32[]{:S(2)}, u32[]{:S(2)}) collective-permute-start(f32[40,4]{1,0:T(8,128)S(1)} %get-tuple-element.53), channel_id=1, source_target_pairs={{1,0},{2,1},{3,2},{0,3},{5,4},{6,5},{7,6},{4,7},{9,8},{10,9},{11,1... | collective-permute-start | bytes 1928 | tf_op jit(solution)/shard_map/ppermute | solution.py:23
  80.8 1.9 collective-permute-done.10
  82.7 0.1 concatenate.33
  82.9 0.7 slice_add_fusion.4
  83.6 0.9 slice_add_fusion.3
  84.5 0.9 fusion.38
  85.5 1.3 multiply_reduce_fusion.5
  86.7 39.8 %all-reduce.1 = (f32[]{:T(128)}, f32[]{:T(128)}) all-reduce(f32[]{:T(128)} %get-tuple-element.6, f32[]{:T(128)} %get-tuple-element.5), channel_id=1, replica_groups=mesh['lat'=8,'lon'=4] {'lat','lon'}, use_global_device_ids=true, to_apply=%region_5.6 | all-reduce | flops 2 | bytes 16 | tf_op jit(solution)/shard_map/psum | solution.py:109
  131.1 2.6 %collective-permute-start.13 = (f32[4,1024]{1,0:T(4,128)S(1)}, f32[4,1024]{1,0:T(4,128)S(1)}, u32[]{:S(2)}, u32[]{:S(2)}) collective-permute-start(f32[4,1024]{1,0:T(4,128)S(1)} %get-tuple-element.58), channel_id=1, source_target_pairs={{4,0},{8,4},{12,8},{16,12},{20,16},{24,20},{28,24},{0,28},{5,1},{9... | collective-permute-start | bytes 49160 | tf_op jit(solution)/shard_map/ppermute | solution.py:23
  133.8 1.4 collective-permute-done.12
  135.3 2.1 %collective-permute-start.14 = (f32[40,4]{1,0:T(8,128)S(1)}, f32[40,4]{1,0:T(8,128)S(1)}, u32[]{:S(2)}, u32[]{:S(2)}) collective-permute-start(f32[40,4]{1,0:T(8,128)S(1)} %get-tuple-element.52), channel_id=1, source_target_pairs={{0,1},{1,2},{2,3},{3,0},{4,5},{5,6},{6,7},{7,4},{8,9},{9,10},{10,1... | collective-permute-start | bytes 1928 | tf_op jit(solution)/shard_map/ppermute | solution.py:20
  137.5 1.7 collective-permute-start.15
  139.2 1.8 collective-permute-done.14
  140.9 0.4 collective-permute-done.15
  141.3 0.1 concatenate.35
  141.4 0.7 slice_add_fusion.2
  142.2 0.9 slice_add_fusion.1
  143.1 0.9 fusion.4
  144.0 1.2 multiply_reduce_fusion.3
  145.2 40.9 %all-reduce = (f32[]{:T(128)}, f32[]{:T(128)}, f32[1]{0:T(128)}, f32[1]{0:T(128)}, f32[1]{0:T(128)}) all-reduce(f32[]{:T(128)} %get-tuple-element.4, f32[]{:T(128)} %get-tuple-element.3, f32[1]{0:T(128)} %bitcast.10, f32[1]{0:T(128)} %bitcast.9, f32[1]{0:T(128)} %bitcast.8), channel_id=1, replica_groups=mesh['lat'=8,'lon'=4] {'lat','lon'}, use_global_device_ids=true, to_apply=%region_9.10 | all-reduce | flops 5 | bytes 40 | tf_op jit(solution)/shard_map/psum | solution.py:109
  190.1 0.9 multiply_subtract_fusion
  190.9 2.4 %pad_maximum_fusion.7 = f32[3]{0:T(128)} fusion(f32[1]{0:T(128)} %get-tuple-element.14, f32[1]{0:T(128)} %get-tuple-element.15, f32[1]{0:T(128)} %get-tuple-element.16), kind=kLoop, calls=%fused_computation.290 | loop fusion | flops 6 | bytes 24 | tf_op jit(solution)/shard_map/stack | solution.py:133
  (39 shorter events, 1.0 us)
Async XLA Ops:
  1.6 15.0 %copy-start.2 = (f32[32,1024]{1,0:T(8,128)}, f32[32,1024]{1,0:T(8,128)S(1)}, u32[]{:S(2)}) copy-start(f32[32,1024]{1,0:T(8,128)S(1)} %convert_multiply_fusion) | copy-start | bytes 393220
  1.6 14.8 %copy-start.4 = (f32[4,32,1024]{2,1,0:T(8,128)S(1)}, f32[4,32,1024]{2,1,0:T(8,128)}, u32[]{:S(2)}) copy-start(f32[4,32,1024]{2,1,0:T(8,128)} %param.5) | copy-start | bytes 1572868
  1.6 14.7 %copy-start.5 = (f32[32,1024]{1,0:T(8,128)S(1)}, f32[32,1024]{1,0:T(8,128)}, u32[]{:S(2)}) copy-start(f32[32,1024]{1,0:T(8,128)} %param.6) | copy-start | bytes 393220
  1.7 8.1 %collective-permute-start = (f32[4,1024]{1,0:T(4,128)S(1)}, f32[4,1024]{1,0:T(4,128)S(1)}, u32[]{:S(2)}, u32[]{:S(2)}) collective-permute-start(f32[4,1024]{1,0:T(4,128)S(1)} %get-tuple-element.61), channel_id=1, source_target_pairs={{0,4},{4,8},{8,12},{12,16},{16,20},{20,24},{24,28},{28,0},{1,5},{5... | collective-permute-start | bytes 49160 | tf_op jit(solution)/shard_map/ppermute | solution.py:20
  2.2 7.6 %collective-permute-start.1 = (f32[4,1024]{1,0:T(4,128)S(1)}, f32[4,1024]{1,0:T(4,128)S(1)}, u32[]{:S(2)}, u32[]{:S(2)}) collective-permute-start(f32[4,1024]{1,0:T(4,128)S(1)} %get-tuple-element.62), channel_id=1, source_target_pairs={{4,0},{8,4},{12,8},{16,12},{20,16},{24,20},{28,24},{0,28},{5,1},{9... | collective-permute-start | bytes 49160 | tf_op jit(solution)/shard_map/ppermute | solution.py:23
  7.1 9.2 %collective-permute-start.4 = (f32[6,5,1024]{2,1,0:T(8,128)S(1)}, f32[6,5,1024]{2,1,0:T(8,128)S(1)}, u32[]{:S(2)}, u32[]{:S(2)}) collective-permute-start(f32[6,5,1024]{2,1,0:T(8,128)S(1)} %get-tuple-element.45), channel_id=1, source_target_pairs={{0,4},{4,8},{8,12},{12,16},{16,20},{20,24},{24,28},{28,0},{1,5},{5... | collective-permute-start | bytes 368648 | tf_op jit(solution)/shard_map/ppermute | solution.py:20
  7.2 9.2 %collective-permute-start.5 = (f32[6,5,1024]{2,1,0:T(8,128)S(1)}, f32[6,5,1024]{2,1,0:T(8,128)S(1)}, u32[]{:S(2)}, u32[]{:S(2)}) collective-permute-start(f32[6,5,1024]{2,1,0:T(8,128)S(1)} %get-tuple-element.46), channel_id=1, source_target_pairs={{4,0},{8,4},{12,8},{16,12},{20,16},{24,20},{28,24},{0,28},{5,1},{9... | collective-permute-start | bytes 368648 | tf_op jit(solution)/shard_map/ppermute | solution.py:23
  9.9 6.2 %collective-permute-start.2 = (f32[40,4]{1,0:T(8,128)S(1)}, f32[40,4]{1,0:T(8,128)S(1)}, u32[]{:S(2)}, u32[]{:S(2)}) collective-permute-start(f32[40,4]{1,0:T(8,128)S(1)} %get-tuple-element.56), channel_id=1, source_target_pairs={{0,1},{1,2},{2,3},{3,0},{4,5},{5,6},{6,7},{7,4},{8,9},{9,10},{10,1... | collective-permute-start | bytes 1928 | tf_op jit(solution)/shard_map/ppermute | solution.py:20
  12.2 4.0 %collective-permute-start.3 = (f32[40,4]{1,0:T(8,128)S(1)}, f32[40,4]{1,0:T(8,128)S(1)}, u32[]{:S(2)}, u32[]{:S(2)}) collective-permute-start(f32[40,4]{1,0:T(8,128)S(1)} %get-tuple-element.55), channel_id=1, source_target_pairs={{1,0},{2,1},{3,2},{0,3},{5,4},{6,5},{7,6},{4,7},{9,8},{10,9},{11,1... | collective-permute-start | bytes 1928 | tf_op jit(solution)/shard_map/ppermute | solution.py:23
  16.3 4.2 %copy-start = (f32[40,1032]{1,0:T(8,128)}, f32[40,1032]{1,0:T(8,128)S(1)}, u32[]{:S(2)}) copy-start(f32[40,1032]{1,0:T(8,128)S(1)} %concatenate.28) | copy-start | bytes 495364
  16.7 8.6 %collective-permute-start.6 = (f32[6,42,5]{2,1,0:T(8,128)S(1)}, f32[6,42,5]{2,1,0:T(8,128)S(1)}, u32[]{:S(2)}, u32[]{:S(2)}) collective-permute-start(f32[6,42,5]{2,1,0:T(8,128)S(1)} %get-tuple-element.44), channel_id=1, source_target_pairs={{0,1},{1,2},{2,3},{3,0},{4,5},{5,6},{6,7},{7,4},{8,9},{9,10},{10,1... | collective-permute-start | bytes 15128 | tf_op jit(solution)/shard_map/ppermute | solution.py:20
  18.1 8.5 %collective-permute-start.7 = (f32[6,42,5]{2,1,0:T(8,128)S(1)}, f32[6,42,5]{2,1,0:T(8,128)S(1)}, u32[]{:S(2)}, u32[]{:S(2)}) collective-permute-start(f32[6,42,5]{2,1,0:T(8,128)S(1)} %get-tuple-element.43), channel_id=1, source_target_pairs={{1,0},{2,1},{3,2},{0,3},{5,4},{6,5},{7,6},{4,7},{9,8},{10,9},{11,1... | collective-permute-start | bytes 15128 | tf_op jit(solution)/shard_map/ppermute | solution.py:23
  27.5 0.9 copy-start.1
  30.2 0.9 copy-start.3
  72.8 4.1 %collective-permute-start.8 = (f32[4,1024]{1,0:T(4,128)S(1)}, f32[4,1024]{1,0:T(4,128)S(1)}, u32[]{:S(2)}, u32[]{:S(2)}) collective-permute-start(f32[4,1024]{1,0:T(4,128)S(1)} %get-tuple-element.59), channel_id=1, source_target_pairs={{0,4},{4,8},{8,12},{12,16},{16,20},{20,24},{24,28},{28,0},{1,5},{5... | collective-permute-start | bytes 49160 | tf_op jit(solution)/shard_map/ppermute | solution.py:20
  72.8 4.1 %collective-permute-start.9 = (f32[4,1024]{1,0:T(4,128)S(1)}, f32[4,1024]{1,0:T(4,128)S(1)}, u32[]{:S(2)}, u32[]{:S(2)}) collective-permute-start(f32[4,1024]{1,0:T(4,128)S(1)} %get-tuple-element.60), channel_id=1, source_target_pairs={{4,0},{8,4},{12,8},{16,12},{20,16},{24,20},{28,24},{0,28},{5,1},{9... | collective-permute-start | bytes 49160 | tf_op jit(solution)/shard_map/ppermute | solution.py:23
  77.0 5.7 %collective-permute-start.10 = (f32[40,4]{1,0:T(8,128)S(1)}, f32[40,4]{1,0:T(8,128)S(1)}, u32[]{:S(2)}, u32[]{:S(2)}) collective-permute-start(f32[40,4]{1,0:T(8,128)S(1)} %get-tuple-element.54), channel_id=1, source_target_pairs={{0,1},{1,2},{2,3},{3,0},{4,5},{5,6},{6,7},{7,4},{8,9},{9,10},{10,1... | collective-permute-start | bytes 1928 | tf_op jit(solution)/shard_map/ppermute | solution.py:20
  77.9 4.8 %collective-permute-start.11 = (f32[40,4]{1,0:T(8,128)S(1)}, f32[40,4]{1,0:T(8,128)S(1)}, u32[]{:S(2)}, u32[]{:S(2)}) collective-permute-start(f32[40,4]{1,0:T(8,128)S(1)} %get-tuple-element.53), channel_id=1, source_target_pairs={{1,0},{2,1},{3,2},{0,3},{5,4},{6,5},{7,6},{4,7},{9,8},{10,9},{11,1... | collective-permute-start | bytes 1928 | tf_op jit(solution)/shard_map/ppermute | solution.py:23
  131.1 4.1 %collective-permute-start.12 = (f32[4,1024]{1,0:T(4,128)S(1)}, f32[4,1024]{1,0:T(4,128)S(1)}, u32[]{:S(2)}, u32[]{:S(2)}) collective-permute-start(f32[4,1024]{1,0:T(4,128)S(1)} %get-tuple-element.57), channel_id=1, source_target_pairs={{0,4},{4,8},{8,12},{12,16},{16,20},{20,24},{24,28},{28,0},{1,5},{5... | collective-permute-start | bytes 49160 | tf_op jit(solution)/shard_map/ppermute | solution.py:20
  131.1 4.1 %collective-permute-start.13 = (f32[4,1024]{1,0:T(4,128)S(1)}, f32[4,1024]{1,0:T(4,128)S(1)}, u32[]{:S(2)}, u32[]{:S(2)}) collective-permute-start(f32[4,1024]{1,0:T(4,128)S(1)} %get-tuple-element.58), channel_id=1, source_target_pairs={{4,0},{8,4},{12,8},{16,12},{20,16},{24,20},{28,24},{0,28},{5,1},{9... | collective-permute-start | bytes 49160 | tf_op jit(solution)/shard_map/ppermute | solution.py:23
  135.3 5.6 %collective-permute-start.14 = (f32[40,4]{1,0:T(8,128)S(1)}, f32[40,4]{1,0:T(8,128)S(1)}, u32[]{:S(2)}, u32[]{:S(2)}) collective-permute-start(f32[40,4]{1,0:T(8,128)S(1)} %get-tuple-element.52), channel_id=1, source_target_pairs={{0,1},{1,2},{2,3},{3,0},{4,5},{5,6},{6,7},{7,4},{8,9},{9,10},{10,1... | collective-permute-start | bytes 1928 | tf_op jit(solution)/shard_map/ppermute | solution.py:20
  137.5 3.8 %collective-permute-start.15 = (f32[40,4]{1,0:T(8,128)S(1)}, f32[40,4]{1,0:T(8,128)S(1)}, u32[]{:S(2)}, u32[]{:S(2)}) collective-permute-start(f32[40,4]{1,0:T(8,128)S(1)} %get-tuple-element.51), channel_id=1, source_target_pairs={{1,0},{2,1},{3,2},{0,3},{5,4},{6,5},{7,6},{4,7},{9,8},{10,9},{11,1... | collective-permute-start | bytes 1928 | tf_op jit(solution)/shard_map/ppermute | solution.py:23
where the time goes:
time: 194 us; the launch traced here: 193 us
  blocking collectives  120 us (62%)
  starting transfers between devices  27.4 us (14%)
  other arithmetic  18.5 us (10%)
  waiting for transfers between devices  14.7 us (8%)
  between operations  10.7 us (6%)
  local copies, waits for them, and re-layouts  2.18 us (1%)
    psum x3, blocking collectives, products(): lax.psum((jnp.sum(r * u), jnp.sum(w * u), jnp.sum(r * r)), ('lat', 'lon'))  120 us
    ppermute x8, starting transfers between devices, padded_2(): lax.ppermute(lax.slice_in_dim(block, 0, width, axis=dim), axis, backward)  20 us
    ppermute x8, waiting for transfers between devices, padded_2(): lax.ppermute(lax.slice_in_dim(block, block.shape[dim] - width, None, axis...  12.9 us
    add x9, other arithmetic, chebyshev(): z = shrink(z, by) + step  7.79 us
    ppermute x8, starting transfers between devices, padded_2(): lax.ppermute(lax.slice_in_dim(block, block.shape[dim] - width, None, axis...  7.47 us
  transfers between devices with their start and end apart: 16, of which 9 were waited for; matrix products, arithmetic and copies ran while one was open for 1% of the time, Pallas kernels for 0%

commit v1 on v0

v1 whole, which is shorter than its diff:
```python
import functools

import jax
import jax.numpy as jnp
from jax import lax
from jax.experimental import pallas as pl
from jax.experimental.pallas import tpu as pltpu
from jax.sharding import PartitionSpec as P

DEG = 4
ITERS = 3
LOW_EIG = 0.25
HIGH_EIG = 20.5
SHIFT = 0.8
LANES = 128
HALO = 16
MESH = pl.DeviceIdType.MESH
DIRS = [(a, b) for a in (-1, 0, 1) for b in (-1, 0, 1) if (a, b) != (0, 0)]


def level_factors():
    theta = (HIGH_EIG + LOW_EIG) / 2.0
    delta = (HIGH_EIG - LOW_EIG) / 2.0
    sigma = theta / delta
    rho = 1.0 / sigma
    out = []
    for _ in range(DEG - 1):
        rho_new = 1.0 / (2.0 * sigma - rho)
        out.append((rho_new * rho, 2.0 * rho_new / delta))
        rho = rho_new
    return theta, out


def scalars(h, g):
    c = SHIFT
    ht = [h[k + 1] + c * h[k] for k in range(len(h) - 1)]

    def form(a, t):
        total = None
        for k in range(2 * len(a) - 1):
            pairs = None
            for i in range(len(a)):
                j = k - i
                if 0 <= j < len(a) and i <= j:
                    term = a[i] * a[j]
                    if i != j:
                        term = term + term
                    pairs = term if pairs is None else pairs + term
            pairs = pairs * t[k]
            total = pairs if total is None else total + pairs
        return total

    one = jnp.ones_like(h[0])
    zero = jnp.zeros_like(h[0])
    a = [one]
    b = [one]
    gamma = h[0]
    norms = [g[0]]
    alpha = gamma / ht[0]
    x = [zero] * ITERS
    beta = zero
    for k in range(ITERS):
        if k > 0:
            b = [a[i] + (beta * b[i] if i < len(b) else 0.0) for i in range(len(a))]
        for i in range(len(b)):
            x[i] = x[i] + alpha * b[i]
        tb = [
            (b[i - 1] if i > 0 else zero) + (c * b[i] if i < len(b) else zero)
            for i in range(len(b) + 1)
        ]
        a = [(a[i] if i < len(a) else zero) - alpha * tb[i] for i in range(len(tb))]
        if k < ITERS - 1:
            gamma_new = form(a, h)
            dlt = form(a, ht)
            norms.append(form(a, g))
            beta = gamma_new / gamma
            alpha = gamma_new / (dlt - beta * gamma_new / alpha)
            gamma = gamma_new
    return x, a, norms


def kernel(
    nlat, nlon, rhs_in, coef_in, extra_in, mask_in, x_out, r_out, n_out,
    B, C, E, M, K, V, U, S, Z, G, GL, GZ, T2,
    loc_sem, snd, rcv, lat_s, lat_r, lon_s, lon_r,
):
    rows, cols = rhs_in.shape
    R = rows + 2 * HALO
    W = cols + 2 * LANES
    NC = W // LANES
    ilat = lax.axis_index("lat")
    ilon = lax.axis_index("lon")

    mid = (pl.ds(HALO, rows), pl.ds(LANES, cols))
    local = [
        pltpu.make_async_copy(coef_in, C.at[:, mid[0], mid[1]], loc_sem.at[0]),
        pltpu.make_async_copy(mask_in, M.at[mid[0], mid[1]], loc_sem.at[1]),
        pltpu.make_async_copy(extra_in, E.at[mid[0], mid[1]], loc_sem.at[2]),
        pltpu.make_async_copy(rhs_in, B.at[mid[0], mid[1]], loc_sem.at[3]),
    ]
    for cp in local:
        cp.start()

    def lat_at(d):
        return lax.rem(ilat + d + nlat, nlat)

    def lon_at(d):
        return lax.rem(ilon + d + nlon, nlon)

    barrier = pltpu.get_barrier_semaphore()
    count = 0
    for d in range(1, nlat):
        pl.semaphore_signal(barrier, inc=1, device_id={"lat": lat_at(d)}, device_id_type=MESH)
        count += 1
    for d in range(1, nlon):
        pl.semaphore_signal(barrier, inc=1, device_id={"lon": lon_at(d)}, device_id_type=MESH)
        count += 1
    for a, b in DIRS:
        if a and b:
            pl.semaphore_signal(
                barrier, inc=1, device_id={"lat": lat_at(a), "lon": lon_at(b)}, device_id_type=MESH
            )
            count += 1
    pl.semaphore_wait(barrier, count)

    def region(d, size, pad, width):
        if d == 0:
            return pad, pad, size
        if d > 0:
            return pad + size - width, 0, width
        return pad, pad + size, width

    sends = []
    for f in range(4):
        local[f].wait()
        for i, (a, b) in enumerate(DIRS):
            rs, rd, rn = region(a, rows, HALO, HALO)
            cs, cd, cn = region(b, cols, LANES, LANES)
            ref = (C, M, E, B)[f]
            lead = (slice(None),) if f == 0 else ()
            where = {}
            if a:
                where["lat"] = lat_at(a)
            if b:
                where["lon"] = lon_at(b)
            cp = pltpu.make_async_remote_copy(
                src_ref=ref.at[(*lead, pl.ds(rs, rn), pl.ds(cs, cn))],
                dst_ref=ref.at[(*lead, pl.ds(rd, rn), pl.ds(cd, cn))],
                send_sem=snd.at[i, f],
                recv_sem=rcv.at[i, f],
                device_id=where,
                device_id_type=MESH,
            )
            cp.start()
            sends.append(cp)
    for cp in sends:
        cp.wait_recv()

    lane = lax.broadcasted_iota(jnp.int32, (R, LANES), 1)
    first = lane == 0
    last = lane == LANES - 1

    def cs_of(j):
        return pl.ds(pl.multiple_of(j * LANES, LANES), LANES)

    def neighbours(j):
        return lax.rem(j + NC - 1, NC), lax.rem(j + 1, NC)

    def east(c, e):
        return jnp.where(last, pltpu.roll(e, LANES - 1, 1), pltpu.roll(c, LANES - 1, 1))

    def west(c, w):
        return jnp.where(first, pltpu.roll(w, 1, 1), pltpu.roll(c, 1, 1))

    def north(a):
        return pltpu.roll(a, R - 1, 0)

    def south(a):
        return pltpu.roll(a, 1, 0)

    grow = lax.broadcasted_iota(jnp.int32, (R, LANES), 0) + (ilat * rows - HALO)
    keep = jnp.where((grow == nlat * rows - 1) | (grow == -1), 0.0, 1.0).astype(jnp.float32)

    @pl.loop(0, NC)
    def _(j):
        wj, ej = neighbours(j)
        m = M[:, cs_of(j)].astype(jnp.float32)
        me = east(m, M[:, cs_of(ej)].astype(jnp.float32))
        mw = west(m, M[:, cs_of(wj)].astype(jnp.float32))
        mk = m * keep
        K[1, :, cs_of(j)] = C[0, :, cs_of(j)] * m * me
        K[6, :, cs_of(j)] = C[1, :, cs_of(j)] * mk * north(m)
        K[9, :, cs_of(j)] = C[2, :, cs_of(j)] * mk * north(me)
        K[10, :, cs_of(j)] = C[3, :, cs_of(j)] * mk * north(mw)
        V[0, :, cs_of(j)] = B[:, cs_of(j)] * m

    @pl.loop(0, NC)
    def _(j):
        wj, ej = neighbours(j)
        le = K[1, :, cs_of(j)]
        wle = west(le, K[1, :, cs_of(wj)])
        ln = K[6, :, cs_of(j)]
        sln = south(ln)
        lne = K[9, :, cs_of(j)]
        wlne = west(lne, K[9, :, cs_of(wj)])
        lnw = K[10, :, cs_of(j)]
        elnw = east(lnw, K[10, :, cs_of(ej)])
        K[2, :, cs_of(j)] = wle
        K[3, :, cs_of(j)] = sln
        K[4, :, cs_of(j)] = south(lne)
        K[5, :, cs_of(j)] = south(lnw)
        K[7, :, cs_of(j)] = wlne
        K[8, :, cs_of(j)] = elnw
        d = E[:, cs_of(j)] + le + wle + ln + sln
        K[0, :, cs_of(j)] = d + lne + south(wlne) + lnw + south(elnw)

    def image(read, j):
        wj, ej = neighbours(j)
        v = read(j)
        ve = east(v, read(ej))
        vw = west(v, read(wj))

        def k(n):
            return K[n, :, cs_of(j)]

        p = k(3) * v + k(4) * ve + k(5) * vw
        q = k(6) * v + k(7) * vw + k(8) * ve
        out = k(0) * v - k(1) * ve - k(2) * vw - north(p) - south(q)
        return v, out

    theta, factors = level_factors()

    @pl.loop(0, ITERS)
    def _(it):
        @pl.loop(0, NC)
        def _(j):
            v, av = image(lambda t: V[it, :, cs_of(t)], j)
            z = v * (1.0 / theta)
            step = factors[0][0] * z + factors[0][1] * (v - av * (1.0 / theta))
            S[:, cs_of(j)] = step
            Z[0, :, cs_of(j)] = z + step

        for level in range(1, DEG - 1):
            src = (level - 1) % 2

            @pl.loop(0, NC)
            def _(j):
                z, az = image(lambda t: Z[src, :, cs_of(t)], j)
                qq = V[it, :, cs_of(j)] - az
                step = factors[level][0] * S[:, cs_of(j)] + factors[level][1] * qq
                if level < DEG - 2:
                    S[:, cs_of(j)] = step
                    Z[1 - src, :, cs_of(j)] = z + step
                else:
                    U[it, :, cs_of(j)] = z + step

        @pl.loop(0, NC)
        def _(j):
            _, au = image(lambda t: U[it, :, cs_of(t)], j)
            V[it + 1, :, cs_of(j)] = au - SHIFT * V[it, :, cs_of(j)]

    hpairs = [((k + 1) // 2, k // 2) for k in range(2 * ITERS)]
    gpairs = [(k // 2, (k + 1) // 2) for k in range(2 * ITERS - 1)]

    def own(ref, n, j):
        return ref[n, pl.ds(HALO, rows), cs_of(j)]

    def fold(a):
        return jnp.sum(a.reshape(rows // 8, 8, LANES), axis=0)

    def add(j, acc):
        v = [own(V, n, j) for n in range(ITERS + 1)]
        u = [own(U, n, j) for n in range(ITERS)]
        new = [fold(v[a] * u[b]) for a, b in hpairs] + [fold(v[a] * v[b]) for a, b in gpairs]
        return tuple(p + q for p, q in zip(acc, new))

    nsum = len(hpairs) + len(gpairs)
    acc = lax.fori_loop(
        1, NC - 1, add, tuple(jnp.zeros((8, LANES), jnp.float32) for _ in range(nsum))
    )
    T2[...] = jnp.zeros_like(T2)
    for n, a in enumerate(acc):
        T2[n : n + 1, :] = jnp.sum(a, axis=0, keepdims=True)
    lo = T2[0:8, :]
    hi = T2[8:16, :]
    lo = lo + pltpu.roll(lo, LANES // 2, 1)
    hi = hi + pltpu.roll(hi, LANES // 2, 1)
    half = lax.broadcasted_iota(jnp.int32, (8, LANES), 1) < LANES // 2
    part = jnp.where(half, lo, hi)

    def exchange(part, slot, buf, axis, count, me, at, ssem, rsem):
        G[slot] = part
        buf[me] = part
        cps = []
        for d in range(1, count):
            cp = pltpu.make_async_remote_copy(
                src_ref=G.at[slot],
                dst_ref=buf.at[me],
                send_sem=ssem.at[d],
                recv_sem=rsem.at[d],
                device_id={axis: at(d)},
                device_id_type=MESH,
            )
            cp.start()
            cps.append(cp)
        for cp in cps:
            cp.wait_recv()
        total = buf[0]
        for n in range(1, count):
            total = total + buf[n]
        return total, cps

    total, c1 = exchange(part, 0, GL, "lat", nlat, ilat, lat_at, lat_s, lat_r)
    total, c2 = exchange(total, 1, GZ, "lon", nlon, ilon, lon_at, lon_s, lon_r)

    for n, t in enumerate((jnp.where(half, total, 0.0), jnp.where(half, 0.0, total))):
        s = jnp.sum(t, axis=1, keepdims=True)
        T2[8 * n : 8 * n + 8, :] = jnp.broadcast_to(s, (8, LANES))
    sums = [T2[n : n + 1, :] for n in range(nsum)]
    xs, rs, norms = scalars(sums[: len(hpairs)], sums[len(hpairs) :])

    @pl.loop(0, NC - 2)
    def _(j):
        x = xs[0] * own(U, 0, j + 1)
        for n in range(1, ITERS):
            x = x + xs[n] * own(U, n, j + 1)
        x_out[:, cs_of(j)] = x
        r = rs[0] * own(V, 0, j + 1)
        for n in range(1, ITERS + 1):
            r = r + rs[n] * own(V, n, j + 1)
        r_out[:, cs_of(j)] = r

    for n in range(ITERS):
        n_out[n] = norms[n][0, 0]
    for cp in sends + c1 + c2:
        cp.wait_send()


def solution(mesh):
    nlat = mesh.shape["lat"]
    nlon = mesh.shape["lon"]

    def body(right_side, coefficients, extra, land_mask):
        rows, cols = right_side.shape
        R, W = rows + 2 * HALO, cols + 2 * LANES
        f32 = jnp.float32
        return pl.pallas_call(
            functools.partial(kernel, nlat, nlon),
            out_shape=(
                jax.ShapeDtypeStruct((rows, cols), f32),
                jax.ShapeDtypeStruct((rows, cols), f32),
                jax.ShapeDtypeStruct((ITERS,), f32),
            ),
            in_specs=[pl.BlockSpec(memory_space=pl.ANY)] * 4,
            out_specs=(
                pl.BlockSpec(memory_space=pltpu.VMEM),
                pl.BlockSpec(memory_space=pltpu.VMEM),
                pl.BlockSpec(memory_space=pltpu.SMEM),
            ),
            scratch_shapes=[
                pltpu.VMEM((R, W), f32),
                pltpu.VMEM((4, R, W), f32),
                pltpu.VMEM((R, W), f32),
                pltpu.VMEM((R, W), jnp.int32),
                pltpu.VMEM((11, R, W), f32),
                pltpu.VMEM((ITERS + 1, R, W), f32),
                pltpu.VMEM((ITERS, R, W), f32),
                pltpu.VMEM((R, W), f32),
                pltpu.VMEM((2, R, W), f32),
                pltpu.VMEM((2, 8, LANES), f32),
                pltpu.VMEM((nlat, 8, LANES), f32),
                pltpu.VMEM((nlon, 8, LANES), f32),
                pltpu.VMEM((16, LANES), f32),
                pltpu.SemaphoreType.DMA((4,)),
                pltpu.SemaphoreType.DMA((8, 4)),
                pltpu.SemaphoreType.DMA((8, 4)),
                pltpu.SemaphoreType.DMA((nlat,)),
                pltpu.SemaphoreType.DMA((nlat,)),
                pltpu.SemaphoreType.DMA((nlon,)),
                pltpu.SemaphoreType.DMA((nlon,)),
            ],
            compiler_params=pltpu.CompilerParams(
                collective_id=0, has_side_effects=True, vmem_limit_bytes=32 * 1024 * 1024
            ),
        )(right_side, coefficients, extra, land_mask)

    return jax.shard_map(
        body,
        mesh=mesh,
        in_specs=(P("lat", "lon"), P(None, "lat", "lon"), P("lat", "lon"), P("lat", "lon")),
        out_specs=(P("lat", "lon"), P("lat", "lon"), P()),
        check_vma=False,
    )
```

time: 194 us -> 52.2 us (0.27)
  blocking collectives: 120 us -> 0 us
  Pallas kernels: 0 us -> 45.7 us
  starting transfers between devices: 27.4 us -> 0 us
  other arithmetic: 18.5 us -> 0 us
  waiting for transfers between devices: 14.7 us -> 0 us
  between operations: 10.7 us -> 0.65 us
  local copies, waits for them, and re-layouts: 2.18 us -> 5.57 us
    psum x3 -> x0, blocking collectives: 120 us -> none  [products(): lax.psum((jnp.sum(r * u), jnp.sum(w * u), jnp.sum(r * r)), ('lat', 'lon'))]
    pallas_call x0 -> x1, Pallas kernels: none -> 45.7 us  [body(): pl.pallas_call(functools.partial(kernel, nlat, nlon), out_shape=(jax.Shap...]
    ppermute x16 -> x0, starting transfers between devices: 27.4 us -> none  [the longest x8 20 us: padded_2(): lax.ppermute(lax.slice_in_dim(block, 0, width, axis=dim), axis, backward)]
    ppermute x16 -> x0, waiting for transfers between devices: 14.7 us -> none  [the longest x8 12.9 us: padded_2(): lax.ppermute(lax.slice_in_dim(block, block.shape[dim] - width, None, axis...]
    add x9 -> x0, other arithmetic: 7.79 us -> none  [chebyshev(): z = shrink(z, by) + step]
    unnamed x12 -> x11, local copies, waits for them, and re-layouts: 0.47 us -> 5.57 us
    reduce_sum x3 -> x0, other arithmetic: 3.68 us -> none  [products(): jnp.sum(w * u)]
    another operation x1 -> x0, other arithmetic: 2.4 us -> none  [on_device(): return (x, r, jnp.stack(norms))]
  transfers between devices with their start and end apart: 16 -> 0, of which waited for: 9 -> 0; matrix products, arithmetic and copies ran while one was open for 1% -> 0% of each run, Pallas kernels for 0% -> 0%
where the time goes in v1:
time: 52.2 us; the launch traced here: 52 us
  Pallas kernels  45.7 us (88%)
  local copies, waits for them, and re-layouts  5.57 us (11%)
  between operations  0.65 us (1%)
    pallas_call x1, Pallas kernels, body(): pl.pallas_call(functools.partial(kernel, nlat, nlon), out_shape=(jax.Shap...  45.7 us
    unnamed x11, local copies, waits for them, and re-layouts  5.57 us

profile of v1, /device:TPU:0, one launch (start us, length us, event | category | flops | bytes accessed | tf_op | source)
XLA Modules:
  0.0 52.0 jit_solution(3138267472936591629)
XLA Ops:
  0.6 0.0 copy-start
  0.6 1.0 %copy-done = f32[4,32,1024]{2,1,0:T(8,128)S(1)} copy-done((f32[4,32,1024]{2,1,0:T(8,128)S(1)}, f32[4,32,1024]{2,1,0:T(8,128)}, u32[]{:S(2)}) %copy-start) | copy-done | bytes 524312
  1.7 0.0 copy-start.1
  1.7 0.9 %copy-done.1 = f32[32,1024]{1,0:T(8,128)S(1)} copy-done((f32[32,1024]{1,0:T(8,128)S(1)}, f32[32,1024]{1,0:T(8,128)}, u32[]{:S(2)}) %copy-start.1) | copy-done | bytes 131096
  2.6 0.0 copy-start.2
  2.6 0.9 %copy-done.2 = f32[32,1024]{1,0:T(8,128)S(1)} copy-done((f32[32,1024]{1,0:T(8,128)S(1)}, f32[32,1024]{1,0:T(8,128)}, u32[]{:S(2)}) %copy-start.2) | copy-done | bytes 131096
  3.5 0.0 copy-start.3
  3.5 0.9 %copy-done.3 = s32[32,1024]{1,0:T(8,128)S(1)} copy-done((s32[32,1024]{1,0:T(8,128)S(1)}, s32[32,1024]{1,0:T(8,128)}, u32[]{:S(2)}) %copy-start.3) | copy-done | bytes 131096
  4.4 45.7 %shard_map.67 = (f32[32,1024]{1,0:T(8,128)S(1)}, f32[32,1024]{1,0:T(8,128)S(1)}, f32[3]{0:T(128)S(1)}) custom-call(f32[32,1024]{1,0:T(8,128)S(1)} %copy-done.1, f32[4,32,1024]{2,1,0:T(8,128)S(1)} %copy-done, f32[32,1024]{1,0:T(8,128)S(1)} %copy-done.2, s32[32,1024]{1,0:T(8,128)S(1)} %copy-done.3), custom_call_target="tpu_custom_call" | custom-call | tf_op jit(solution)/shard_map/pallas_call | solution.py:347
  50.1 0.7 %copy.10 = f32[32,1024]{1,0:T(8,128)} copy(f32[32,1024]{1,0:T(8,128)S(1)} %get-tuple-element.6) | data formatting | bytes 262144
  50.8 0.7 %copy.11 = f32[32,1024]{1,0:T(8,128)} copy(f32[32,1024]{1,0:T(8,128)S(1)} %get-tuple-element.7) | data formatting | bytes 262144
  51.5 0.5 copy.12
Async XLA Ops:
  0.6 1.0 %copy-start = (f32[4,32,1024]{2,1,0:T(8,128)S(1)}, f32[4,32,1024]{2,1,0:T(8,128)}, u32[]{:S(2)}) copy-start(f32[4,32,1024]{2,1,0:T(8,128)} %coef_in.1) | copy-start | bytes 1572868
  1.7 0.9 %copy-start.1 = (f32[32,1024]{1,0:T(8,128)S(1)}, f32[32,1024]{1,0:T(8,128)}, u32[]{:S(2)}) copy-start(f32[32,1024]{1,0:T(8,128)} %rhs_in.1) | copy-start | bytes 393220
  2.6 0.9 %copy-start.2 = (f32[32,1024]{1,0:T(8,128)S(1)}, f32[32,1024]{1,0:T(8,128)}, u32[]{:S(2)}) copy-start(f32[32,1024]{1,0:T(8,128)} %extra_in.1) | copy-start | bytes 393220
  3.5 0.9 %copy-start.3 = (s32[32,1024]{1,0:T(8,128)S(1)}, s32[32,1024]{1,0:T(8,128)}, u32[]{:S(2)}) copy-start(s32[32,1024]{1,0:T(8,128)} %mask_in.1) | copy-start | bytes 393220

commit v2 on v1

--- a/solution.py
+++ b/solution.py
@@ -14,6 +14,9 @@
 SHIFT = 0.8
 LANES = 128
 HALO = 16
+STRIP = 16
+FIELDS = 7
+PAIRS = (FIELDS + 1) // 2
 MESH = pl.DeviceIdType.MESH
 DIRS = [(a, b) for a in (-1, 0, 1) for b in (-1, 0, 1) if (a, b) != (0, 0)]
 
@@ -81,7 +84,7 @@
 
 def kernel(
     nlat, nlon, rhs_in, coef_in, extra_in, mask_in, x_out, r_out, n_out,
-    B, C, E, M, K, V, U, S, Z, G, GL, GZ, T2,
+    B, C, E, M, K, V, U, VC, UC, S, Z, SP, RP, SR, RR, G, GL, GZ, T2,
     loc_sem, snd, rcv, lat_s, lat_r, lon_s, lon_r,
 ):
     rows, cols = rhs_in.shape
@@ -90,6 +93,9 @@
     NC = W // LANES
     ilat = lax.axis_index("lat")
     ilon = lax.axis_index("lon")
+
+    def cs_of(j):
+        return slice(j * LANES, (j + 1) * LANES)
 
     mid = (pl.ds(HALO, rows), pl.ds(LANES, cols))
     local = [
@@ -121,59 +127,122 @@
                 barrier, inc=1, device_id={"lat": lat_at(a), "lon": lon_at(b)}, device_id_type=MESH
             )
             count += 1
+    for cp in local:
+        cp.wait()
+
+    def field(f, rws, cls):
+        if f < 4:
+            return C[f, rws, cls]
+        if f == 4:
+            return E[rws, cls]
+        if f == 5:
+            return B[rws, cls]
+        return M[rws, cls].astype(jnp.float32)
+
+    def put(f, rws, cls, value):
+        if f < 4:
+            C[f, rws, cls] = value
+        elif f == 4:
+            E[rws, cls] = value
+        elif f == 5:
+            B[rws, cls] = value
+        else:
+            M[rws, cls] = value.astype(jnp.int32)
+
+    own_rows = slice(HALO, HALO + rows)
+    slot = lax.broadcasted_iota(jnp.int32, (rows, LANES), 1) // STRIP
+    for side, chunk in ((0, 1), (1, NC - 2)):
+        strip = jnp.zeros((rows, LANES), jnp.float32)
+        for f in range(FIELDS):
+            turn = (STRIP * f + side * STRIP) % LANES
+            a = field(f, own_rows, cs_of(chunk))
+            a = pltpu.roll(a, turn, 1) if turn else a
+            strip = jnp.where(slot == f, a, strip)
+        SP[side] = strip
+    upper = lax.broadcasted_iota(jnp.int32, (8, cols), 0) >= 4
+    inner = slice(LANES, LANES + cols)
+    near = (slice(HALO + 8, HALO + 16), slice(HALO + rows - 16, HALO + rows - 8))
+    for side in (0, 1):
+        for t in range(PAIRS):
+            a = field(2 * t, near[side], inner)
+            if 2 * t + 1 < FIELDS:
+                b = pltpu.roll(field(2 * t + 1, near[side], inner), 4, 0)
+                a = jnp.where(upper, a, b) if side else jnp.where(upper, b, a)
+            SR[side, t] = a
     pl.semaphore_wait(barrier, count)
 
-    def region(d, size, pad, width):
-        if d == 0:
-            return pad, pad, size
-        if d > 0:
-            return pad + size - width, 0, width
-        return pad, pad + size, width
-
     sends = []
-    for f in range(4):
-        local[f].wait()
-        for i, (a, b) in enumerate(DIRS):
-            rs, rd, rn = region(a, rows, HALO, HALO)
-            cs, cd, cn = region(b, cols, LANES, LANES)
-            ref = (C, M, E, B)[f]
-            lead = (slice(None),) if f == 0 else ()
-            where = {}
-            if a:
-                where["lat"] = lat_at(a)
-            if b:
-                where["lon"] = lon_at(b)
-            cp = pltpu.make_async_remote_copy(
-                src_ref=ref.at[(*lead, pl.ds(rs, rn), pl.ds(cs, cn))],
-                dst_ref=ref.at[(*lead, pl.ds(rd, rn), pl.ds(cd, cn))],
-                send_sem=snd.at[i, f],
-                recv_sem=rcv.at[i, f],
-                device_id=where,
-                device_id_type=MESH,
-            )
-            cp.start()
-            sends.append(cp)
+
+    def send(src, dst, a, b):
+        i = len(sends)
+        where = {}
+        if a:
+            where["lat"] = lat_at(a)
+        if b:
+            where["lon"] = lon_at(b)
+        cp = pltpu.make_async_remote_copy(
+            src_ref=src, dst_ref=dst, send_sem=snd.at[i], recv_sem=rcv.at[i],
+            device_id=where, device_id_type=MESH,
+        )
+        cp.start()
+        sends.append(cp)
+
+    for a in (-1, 1):
+        side = (a + 1) // 2
+        src = pl.ds(HALO, 8) if a < 0 else pl.ds(HALO + rows - 8, 8)
+        dst = pl.ds(HALO + rows, 8) if a < 0 else pl.ds(HALO - 8, 8)
+        wide = pl.ds(LANES, cols)
+        send(C.at[:, src, wide], C.at[:, dst, wide], a, 0)
+        for ref in (E, B, M):
+            send(ref.at[src, wide], ref.at[dst, wide], a, 0)
+        send(SR.at[side], RR.at[side], a, 0)
+    for b in (-1, 1):
+        side = (b + 1) // 2
+        send(SP.at[side], RP.at[side, pl.ds(HALO, rows)], 0, b)
+        for a in (-1, 1):
+            src = pl.ds(0, HALO) if a < 0 else pl.ds(rows - HALO, HALO)
+            dst = pl.ds(HALO + rows, HALO) if a < 0 else pl.ds(0, HALO)
+            send(SP.at[side, src], RP.at[side, dst], a, b)
     for cp in sends:
         cp.wait_recv()
 
-    lane = lax.broadcasted_iota(jnp.int32, (R, LANES), 1)
-    first = lane == 0
-    last = lane == LANES - 1
-
-    def cs_of(j):
-        return pl.ds(pl.multiple_of(j * LANES, LANES), LANES)
-
-    def neighbours(j):
-        return lax.rem(j + NC - 1, NC), lax.rem(j + 1, NC)
-
-    def east(c, e):
-        return jnp.where(last, pltpu.roll(e, LANES - 1, 1), pltpu.roll(c, LANES - 1, 1))
-
-    def west(c, w):
-        return jnp.where(first, pltpu.roll(w, 1, 1), pltpu.roll(c, 1, 1))
+    every = slice(0, R)
+    for side, chunk in ((0, NC - 1), (1, 0)):
+        strip = RP[side]
+        for f in range(FIELDS):
+            turn = (-STRIP * f - side * STRIP) % LANES
+            put(f, every, cs_of(chunk), pltpu.roll(strip, turn, 1) if turn else strip)
+    far = (slice(R - 8, R), slice(0, 8))
+    for side in (0, 1):
+        for f in range(FIELDS):
+            a = RR[side, f // 2]
+            put(f, far[side], inner, pltpu.roll(a, 4, 0) if f % 2 else a)
+
+    def shifts(read, n):
+        lane = lax.broadcasted_iota(jnp.int32, (n, LANES), 1)
+        first = lane == 0
+        last = lane == LANES - 1
+        memo = {}
+
+        def get(kind, j):
+            j = j % NC
+            if (kind, j) not in memo:
+                if kind == 0:
+                    memo[kind, j] = read(j)
+                else:
+                    memo[kind, j] = pltpu.roll(get(0, j), 1 if kind < 0 else LANES - 1, 1)
+            return memo[kind, j]
+
+        def east(j):
+            return jnp.where(last, get(1, j + 1), get(1, j))
+
+        def west(j):
+            return jnp.where(first, get(-1, j - 1), get(-1, j))
+
+        return (lambda j: get(0, j)), east, west
 
     def north(a):
-        return pltpu.roll(a, R - 1, 0)
+        return pltpu.roll(a, a.shape[0] - 1, 0)
 
     def south(a):
         return pltpu.roll(a, 1, 0)
@@ -181,89 +250,104 @@
     grow = lax.broadcasted_iota(jnp.int32, (R, LANES), 0) + (ilat * rows - HALO)
     keep = jnp.where((grow == nlat * rows - 1) | (grow == -1), 0.0, 1.0).astype(jnp.float32)
 
-    @pl.loop(0, NC)
-    def _(j):
-        wj, ej = neighbours(j)
-        m = M[:, cs_of(j)].astype(jnp.float32)
-        me = east(m, M[:, cs_of(ej)].astype(jnp.float32))
-        mw = west(m, M[:, cs_of(wj)].astype(jnp.float32))
+    mc, mE, mW = shifts(lambda j: M[:, cs_of(j)].astype(jnp.float32), R)
+    for j in range(NC):
+        m = mc(j)
+        me = mE(j)
+        mw = mW(j)
         mk = m * keep
-        K[1, :, cs_of(j)] = C[0, :, cs_of(j)] * m * me
-        K[6, :, cs_of(j)] = C[1, :, cs_of(j)] * mk * north(m)
-        K[9, :, cs_of(j)] = C[2, :, cs_of(j)] * mk * north(me)
-        K[10, :, cs_of(j)] = C[3, :, cs_of(j)] * mk * north(mw)
-        V[0, :, cs_of(j)] = B[:, cs_of(j)] * m
-
-    @pl.loop(0, NC)
-    def _(j):
-        wj, ej = neighbours(j)
-        le = K[1, :, cs_of(j)]
-        wle = west(le, K[1, :, cs_of(wj)])
-        ln = K[6, :, cs_of(j)]
+        K[1][:, cs_of(j)] = C[0, :, cs_of(j)] * m * me
+        K[6][:, cs_of(j)] = C[1, :, cs_of(j)] * mk * north(m)
+        K[9][:, cs_of(j)] = C[2, :, cs_of(j)] * mk * north(me)
+        K[10][:, cs_of(j)] = C[3, :, cs_of(j)] * mk * north(mw)
+        VC[:, cs_of(j)] = B[:, cs_of(j)] * m
+
+    cle, _, wle_of = shifts(lambda j: K[1][:, cs_of(j)], R)
+    clne, _, wlne_of = shifts(lambda j: K[9][:, cs_of(j)], R)
+    clnw, elnw_of, _ = shifts(lambda j: K[10][:, cs_of(j)], R)
+    for j in range(NC):
+        le = cle(j)
+        wle = wle_of(j)
+        ln = K[6][:, cs_of(j)]
         sln = south(ln)
-        lne = K[9, :, cs_of(j)]
-        wlne = west(lne, K[9, :, cs_of(wj)])
-        lnw = K[10, :, cs_of(j)]
-        elnw = east(lnw, K[10, :, cs_of(ej)])
-        K[2, :, cs_of(j)] = wle
-        K[3, :, cs_of(j)] = sln
-        K[4, :, cs_of(j)] = south(lne)
-        K[5, :, cs_of(j)] = south(lnw)
-        K[7, :, cs_of(j)] = wlne
-        K[8, :, cs_of(j)] = elnw
+        lne = clne(j)
+        wlne = wlne_of(j)
+        lnw = clnw(j)
+        elnw = elnw_of(j)
+        K[2][:, cs_of(j)] = wle
+        K[3][:, cs_of(j)] = sln
+        K[4][:, cs_of(j)] = south(lne)
+        K[5][:, cs_of(j)] = south(lnw)
+        K[7][:, cs_of(j)] = wlne
+        K[8][:, cs_of(j)] = elnw
         d = E[:, cs_of(j)] + le + wle + ln + sln
-        K[0, :, cs_of(j)] = d + lne + south(wlne) + lnw + south(elnw)
-
-    def image(read, j):
-        wj, ej = neighbours(j)
-        v = read(j)
-        ve = east(v, read(ej))
-        vw = west(v, read(wj))
-
-        def k(n):
-            return K[n, :, cs_of(j)]
-
-        p = k(3) * v + k(4) * ve + k(5) * vw
-        q = k(6) * v + k(7) * vw + k(8) * ve
-        out = k(0) * v - k(1) * ve - k(2) * vw - north(p) - south(q)
-        return v, out
+        K[0][:, cs_of(j)] = d + lne + south(wlne) + lnw + south(elnw)
 
     theta, factors = level_factors()
 
-    @pl.loop(0, ITERS)
-    def _(it):
-        @pl.loop(0, NC)
-        def _(j):
-            v, av = image(lambda t: V[it, :, cs_of(t)], j)
+    def apply(ref, rws, finish):
+        n = rws.stop - rws.start
+        centre, east, west = shifts(lambda j: ref[rws, cs_of(j)], n)
+        for j in range(NC):
+            v = centre(j)
+            ve = east(j)
+            vw = west(j)
+
+            def k(i):
+                return K[i][rws, cs_of(j)]
+
+            p = k(3) * v + k(4) * ve + k(5) * vw
+            q = k(6) * v + k(7) * vw + k(8) * ve
+            finish(cs_of(j), v, k(0) * v - k(1) * ve - k(2) * vw - north(p) - south(q))
+
+    mine = slice(HALO, HALO + rows)
+
+    def round_of(it, rws):
+        lo = HALO - rws.start
+
+        def level0(cls, v, av):
             z = v * (1.0 / theta)
             step = factors[0][0] * z + factors[0][1] * (v - av * (1.0 / theta))
-            S[:, cs_of(j)] = step
-            Z[0, :, cs_of(j)] = z + step
-
+            S[rws, cls] = step
+            Z[0][rws, cls] = z + step
+
+        apply(VC, rws, level0)
         for level in range(1, DEG - 1):
             src = (level - 1) % 2
 
-            @pl.loop(0, NC)
-            def _(j):
-                z, az = image(lambda t: Z[src, :, cs_of(t)], j)
-                qq = V[it, :, cs_of(j)] - az
-                step = factors[level][0] * S[:, cs_of(j)] + factors[level][1] * qq
+            def inner_level(cls, z, az):
+                qq = VC[rws, cls] - az
+                step = factors[level][0] * S[rws, cls] + factors[level][1] * qq
+                new = z + step
                 if level < DEG - 2:
-                    S[:, cs_of(j)] = step
-                    Z[1 - src, :, cs_of(j)] = z + step
+                    S[rws, cls] = step
+                    Z[1 - src][rws, cls] = new
                 else:
-                    U[it, :, cs_of(j)] = z + step
-
-        @pl.loop(0, NC)
-        def _(j):
-            _, au = image(lambda t: U[it, :, cs_of(t)], j)
-            V[it + 1, :, cs_of(j)] = au - SHIFT * V[it, :, cs_of(j)]
+                    UC[rws, cls] = new
+                    U[it, :, cls] = new[lo : lo + rows]
+
+            apply(Z[src], rws, inner_level)
+
+        def last_level(cls, u, au):
+            new = au - SHIFT * VC[rws, cls]
+            VC[rws, cls] = new
+            V[it + 1, :, cls] = new[lo : lo + rows]
+
+        apply(UC, rws, last_level)
+
+    for j in range(1, NC - 1):
+        V[0, :, cs_of(j)] = VC[mine, cs_of(j)]
+    round_of(0, slice(0, R))
+
+    @pl.loop(1, ITERS)
+    def _(it):
+        round_of(it, slice(8, R - 8))
 
     hpairs = [((k + 1) // 2, k // 2) for k in range(2 * ITERS)]
     gpairs = [(k // 2, (k + 1) // 2) for k in range(2 * ITERS - 1)]
 
     def own(ref, n, j):
-        return ref[n, pl.ds(HALO, rows), cs_of(j)]
+        return ref[n, :, cs_of(j)]
 
     def fold(a):
         return jnp.sum(a.reshape(rows // 8, 8, LANES), axis=0)
@@ -275,9 +359,9 @@
         return tuple(p + q for p, q in zip(acc, new))
 
     nsum = len(hpairs) + len(gpairs)
-    acc = lax.fori_loop(
-        1, NC - 1, add, tuple(jnp.zeros((8, LANES), jnp.float32) for _ in range(nsum))
-    )
+    acc = tuple(jnp.zeros((8, LANES), jnp.float32) for _ in range(nsum))
+    for j in range(1, NC - 1):
+        acc = add(j, acc)
     T2[...] = jnp.zeros_like(T2)
     for n, a in enumerate(acc):
         T2[n : n + 1, :] = jnp.sum(a, axis=0, keepdims=True)
@@ -319,8 +403,7 @@
     sums = [T2[n : n + 1, :] for n in range(nsum)]
     xs, rs, norms = scalars(sums[: len(hpairs)], sums[len(hpairs) :])
 
-    @pl.loop(0, NC - 2)
-    def _(j):
+    for j in range(NC - 2):
         x = xs[0] * own(U, 0, j + 1)
         for n in range(1, ITERS):
             x = x + xs[n] * own(U, n, j + 1)
@@ -362,18 +445,24 @@
                 pltpu.VMEM((4, R, W), f32),
                 pltpu.VMEM((R, W), f32),
                 pltpu.VMEM((R, W), jnp.int32),
-                pltpu.VMEM((11, R, W), f32),
-                pltpu.VMEM((ITERS + 1, R, W), f32),
-                pltpu.VMEM((ITERS, R, W), f32),
+                [pltpu.VMEM((R, W), f32)] * 11,
+                pltpu.VMEM((ITERS + 1, rows, W), f32),
+                pltpu.VMEM((ITERS, rows, W), f32),
                 pltpu.VMEM((R, W), f32),
-                pltpu.VMEM((2, R, W), f32),
+                pltpu.VMEM((R, W), f32),
+                pltpu.VMEM((R, W), f32),
+                [pltpu.VMEM((R, W), f32)] * 2,
+                pltpu.VMEM((2, rows, LANES), f32),
+                pltpu.VMEM((2, R, LANES), f32),
+                pltpu.VMEM((2, PAIRS, 8, cols), f32),
+                pltpu.VMEM((2, PAIRS, 8, cols), f32),
                 pltpu.VMEM((2, 8, LANES), f32),
                 pltpu.VMEM((nlat, 8, LANES), f32),
                 pltpu.VMEM((nlon, 8, LANES), f32),
                 pltpu.VMEM((16, LANES), f32),
                 pltpu.SemaphoreType.DMA((4,)),
-                pltpu.SemaphoreType.DMA((8, 4)),
-                pltpu.SemaphoreType.DMA((8, 4)),
+                pltpu.SemaphoreType.DMA((16,)),
+                pltpu.SemaphoreType.DMA((16,)),
                 pltpu.SemaphoreType.DMA((nlat,)),
                 pltpu.SemaphoreType.DMA((nlat,)),
                 pltpu.SemaphoreType.DMA((nlon,)),

time: 52.2 us -> 34.9 us (0.67)
  Pallas kernels: 45.7 us -> 28.5 us
    pallas_call x1, Pallas kernels: 45.7 us -> 28.5 us  [body(): pl.pallas_call(functools.partial(kernel, nlat, nlon), out_shape=(jax.Shap...]
where the time goes in v2:
time: 34.9 us; the launch traced here: 34.7 us
  Pallas kernels  28.5 us (82%)
  local copies, waits for them, and re-layouts  5.57 us (16%)
  between operations  0.65 us (2%)
    pallas_call x1, Pallas kernels, body(): pl.pallas_call(functools.partial(kernel, nlat, nlon), out_shape=(jax.Shap...  28.5 us
    unnamed x11, local copies, waits for them, and re-layouts  5.57 us

profile of v2, /device:TPU:0, one launch (start us, length us, event | category | flops | bytes accessed | tf_op | source)
XLA Modules:
  0.0 34.7 jit_solution(16982795951495759608)
XLA Ops:
  0.6 0.0 copy-start
  0.6 1.0 %copy-done = f32[4,32,1024]{2,1,0:T(8,128)S(1)} copy-done((f32[4,32,1024]{2,1,0:T(8,128)S(1)}, f32[4,32,1024]{2,1,0:T(8,128)}, u32[]{:S(2)}) %copy-start) | copy-done | bytes 524312
  1.7 0.0 copy-start.1
  1.7 0.9 %copy-done.1 = f32[32,1024]{1,0:T(8,128)S(1)} copy-done((f32[32,1024]{1,0:T(8,128)S(1)}, f32[32,1024]{1,0:T(8,128)}, u32[]{:S(2)}) %copy-start.1) | copy-done | bytes 131096
  2.6 0.0 copy-start.2
  2.6 0.9 %copy-done.2 = f32[32,1024]{1,0:T(8,128)S(1)} copy-done((f32[32,1024]{1,0:T(8,128)S(1)}, f32[32,1024]{1,0:T(8,128)}, u32[]{:S(2)}) %copy-start.2) | copy-done | bytes 131096
  3.5 0.0 copy-start.3
  3.5 0.9 %copy-done.3 = s32[32,1024]{1,0:T(8,128)S(1)} copy-done((s32[32,1024]{1,0:T(8,128)S(1)}, s32[32,1024]{1,0:T(8,128)}, u32[]{:S(2)}) %copy-start.3) | copy-done | bytes 131096
  4.4 28.5 %shard_map.67 = (f32[32,1024]{1,0:T(8,128)S(1)}, f32[32,1024]{1,0:T(8,128)S(1)}, f32[3]{0:T(128)S(1)}) custom-call(f32[32,1024]{1,0:T(8,128)S(1)} %copy-done.1, f32[4,32,1024]{2,1,0:T(8,128)S(1)} %copy-done, f32[32,1024]{1,0:T(8,128)S(1)} %copy-done.2, s32[32,1024]{1,0:T(8,128)S(1)} %copy-done.3), custom_call_target="tpu_custom_call" | custom-call | tf_op jit(solution)/shard_map/pallas_call | solution.py:430
  32.9 0.7 %copy.10 = f32[32,1024]{1,0:T(8,128)} copy(f32[32,1024]{1,0:T(8,128)S(1)} %get-tuple-element.6) | data formatting | bytes 262144
  33.5 0.7 %copy.11 = f32[32,1024]{1,0:T(8,128)} copy(f32[32,1024]{1,0:T(8,128)S(1)} %get-tuple-element.7) | data formatting | bytes 262144
  34.2 0.5 %copy.12 = f32[3]{0:T(128)} copy(f32[3]{0:T(128)S(1)} %get-tuple-element.8) | data formatting | bytes 24
Async XLA Ops:
  0.6 1.0 %copy-start = (f32[4,32,1024]{2,1,0:T(8,128)S(1)}, f32[4,32,1024]{2,1,0:T(8,128)}, u32[]{:S(2)}) copy-start(f32[4,32,1024]{2,1,0:T(8,128)} %coef_in.1) | copy-start | bytes 1572868
  1.7 0.9 %copy-start.1 = (f32[32,1024]{1,0:T(8,128)S(1)}, f32[32,1024]{1,0:T(8,128)}, u32[]{:S(2)}) copy-start(f32[32,1024]{1,0:T(8,128)} %rhs_in.1) | copy-start | bytes 393220
  2.6 0.9 %copy-start.2 = (f32[32,1024]{1,0:T(8,128)S(1)}, f32[32,1024]{1,0:T(8,128)}, u32[]{:S(2)}) copy-start(f32[32,1024]{1,0:T(8,128)} %extra_in.1) | copy-start | bytes 393220
  3.5 0.9 %copy-start.3 = (s32[32,1024]{1,0:T(8,128)S(1)}, s32[32,1024]{1,0:T(8,128)}, u32[]{:S(2)}) copy-start(s32[32,1024]{1,0:T(8,128)} %mask_in.1) | copy-start | bytes 393220

commit v3 on v2

--- a/solution.py
+++ b/solution.py
@@ -14,6 +14,7 @@
 SHIFT = 0.8
 LANES = 128
 HALO = 16
+VMEM_GRANT = 67043328
 STRIP = 16
 FIELDS = 7
 PAIRS = (FIELDS + 1) // 2
@@ -127,8 +128,6 @@
                 barrier, inc=1, device_id={"lat": lat_at(a), "lon": lon_at(b)}, device_id_type=MESH
             )
             count += 1
-    for cp in local:
-        cp.wait()
 
     def field(f, rws, cls):
         if f < 4:
@@ -148,6 +147,37 @@
             B[rws, cls] = value
         else:
             M[rws, cls] = value.astype(jnp.int32)
+
+    pl.semaphore_wait(barrier, count)
+
+    sends = []
+
+    def send(src, dst, a, b):
+        i = len(sends)
+        where = {}
+        if a:
+            where["lat"] = lat_at(a)
+        if b:
+            where["lon"] = lon_at(b)
+        cp = pltpu.make_async_remote_copy(
+            src_ref=src, dst_ref=dst, send_sem=snd.at[i], recv_sem=rcv.at[i],
+            device_id=where, device_id_type=MESH,
+        )
+        cp.start()
+        sends.append(cp)
+
+    wide = pl.ds(LANES, cols)
+    spans = {
+        -1: (pl.ds(HALO, 8), pl.ds(HALO + rows, 8)),
+        1: (pl.ds(HALO + rows - 8, 8), pl.ds(HALO - 8, 8)),
+    }
+    for ref, cp in zip((C, M, E, B), local):
+        cp.wait()
+        for a, (src, dst) in spans.items():
+            if ref is C:
+                send(C.at[:, src, wide], C.at[:, dst, wide], a, 0)
+            else:
+                send(ref.at[src, wide], ref.at[dst, wide], a, 0)
 
     own_rows = slice(HALO, HALO + rows)
     slot = lax.broadcasted_iota(jnp.int32, (rows, LANES), 1) // STRIP
@@ -169,33 +199,6 @@
                 b = pltpu.roll(field(2 * t + 1, near[side], inner), 4, 0)
                 a = jnp.where(upper, a, b) if side else jnp.where(upper, b, a)
             SR[side, t] = a
-    pl.semaphore_wait(barrier, count)
-
-    sends = []
-
-    def send(src, dst, a, b):
-        i = len(sends)
-        where = {}
-        if a:
-            where["lat"] = lat_at(a)
-        if b:
-            where["lon"] = lon_at(b)
-        cp = pltpu.make_async_remote_copy(
-            src_ref=src, dst_ref=dst, send_sem=snd.at[i], recv_sem=rcv.at[i],
-            device_id=where, device_id_type=MESH,
-        )
-        cp.start()
-        sends.append(cp)
-
-    for a in (-1, 1):
-        side = (a + 1) // 2
-        src = pl.ds(HALO, 8) if a < 0 else pl.ds(HALO + rows - 8, 8)
-        dst = pl.ds(HALO + rows, 8) if a < 0 else pl.ds(HALO - 8, 8)
-        wide = pl.ds(LANES, cols)
-        send(C.at[:, src, wide], C.at[:, dst, wide], a, 0)
-        for ref in (E, B, M):
-            send(ref.at[src, wide], ref.at[dst, wide], a, 0)
-        send(SR.at[side], RR.at[side], a, 0)
     for b in (-1, 1):
         side = (b + 1) // 2
         send(SP.at[side], RP.at[side, pl.ds(HALO, rows)], 0, b)
@@ -203,6 +206,9 @@
             src = pl.ds(0, HALO) if a < 0 else pl.ds(rows - HALO, HALO)
             dst = pl.ds(HALO + rows, HALO) if a < 0 else pl.ds(0, HALO)
             send(SP.at[side, src], RP.at[side, dst], a, b)
+    for a in (-1, 1):
+        side = (a + 1) // 2
+        send(SR.at[side], RR.at[side], a, 0)
     for cp in sends:
         cp.wait_recv()
 
@@ -469,7 +475,7 @@
                 pltpu.SemaphoreType.DMA((nlon,)),
             ],
             compiler_params=pltpu.CompilerParams(
-                collective_id=0, has_side_effects=True, vmem_limit_bytes=32 * 1024 * 1024
+                collective_id=0, has_side_effects=True, vmem_limit_bytes=VMEM_GRANT
             ),
         )(right_side, coefficients, extra, land_mask)
 

time: 34.9 us -> 32.1 us (0.920)
  local copies, waits for them, and re-layouts: 5.57 us -> 2.79 us
    unnamed x11 -> x7, local copies, waits for them, and re-layouts: 5.57 us -> 2.79 us
where the time goes in v3:
time: 32.1 us; the launch traced here: 31.9 us
  Pallas kernels  28.5 us (89%)
  local copies, waits for them, and re-layouts  2.79 us (9%)
  between operations  0.65 us (2%)
    pallas_call x1, Pallas kernels, body(): pl.pallas_call(functools.partial(kernel, nlat, nlon), out_shape=(jax.Shap...  28.5 us
    unnamed x7, local copies, waits for them, and re-layouts  2.79 us

profile of v3, /device:TPU:0, one launch (start us, length us, event | category | flops | bytes accessed | tf_op | source)
XLA Modules:
  0.0 31.9 jit_solution(12161550908636816998)
XLA Ops:
  0.6 28.5 %shard_map.67 = (f32[32,1024]{1,0:T(8,128)}, f32[32,1024]{1,0:T(8,128)}, f32[3]{0:T(128)}) custom-call(f32[32,1024]{1,0:T(8,128)} %rhs_in.1, f32[4,32,1024]{2,1,0:T(8,128)} %coef_in.1, f32[32,1024]{1,0:T(8,128)} %extra_in.1, s32[32,1024]{1,0:T(8,128)} %mask_in.1), custom_call_target="tpu_custom_call" | custom-call | tf_op jit(solution)/shard_map/pallas_call | solution.py:436
  29.1 0.0 copy-start
  29.1 1.6 %copy.10 = f32[32,1024]{1,0:T(8,128)} copy(f32[32,1024]{1,0:T(8,128)} %get-tuple-element.6) | data formatting | bytes 262144
  30.7 0.0 copy-done
  30.7 0.0 copy-start.1
  30.7 0.7 %copy.11 = f32[32,1024]{1,0:T(8,128)} copy(f32[32,1024]{1,0:T(8,128)S(1)} %copy-done) | data formatting | bytes 262144
  31.4 0.0 copy-done.1
  31.4 0.5 %copy.12 = f32[3]{0:T(128)} copy(f32[3]{0:T(128)S(1)} %copy-done.1) | data formatting | bytes 24
Async XLA Ops:
  29.1 1.6 %copy-start = (f32[32,1024]{1,0:T(8,128)S(1)}, f32[32,1024]{1,0:T(8,128)}, u32[]{:S(2)}) copy-start(f32[32,1024]{1,0:T(8,128)} %get-tuple-element.7) | copy-start | bytes 393220
  30.7 0.7 %copy-start.1 = (f32[3]{0:T(128)S(1)}, f32[3]{0:T(128)}, u32[]{:S(2)}) copy-start(f32[3]{0:T(128)} %get-tuple-element.8) | copy-start | bytes 40
